TPU v7x, 32 devices: a whole 2x2x4 slice. The times are simulated.
32 devices in a mesh: fld: 2 (over x), col: 4 (over z), row: 4 (over y, core).
Axes of the slice: x: 2, y: 2, z: 4, core: 2. Of those that a mesh axis runs over, the one named last changes fastest.
Arguments:
- u_real: float32 [32, 128, 128, 128], P('fld', None, 'row', 'col'), parts along dimension 0
- u_imag: float32 [32, 128, 128, 128], P('fld', None, 'row', 'col'), parts along dimension 0
- g_filter: float32 [128, 128, 128], P('row', 'col')
Outputs:
- output 1: float32 [32, 128, 128, 128], P('fld', 'row', 'col'), parts along dimension 0
- output 2: float32 [32, 128, 128, 128], P('fld', 'row', 'col'), parts along dimension 0
There are 2 independent parts. A program takes and returns all parts, laid end to end along the dimension named above; an argument that names none is the same for every part.
All inputs are finite; a program needn't handle non-finite values.
Results may differ from a plain program's by a relative error of at most 0.001.
Values are sent between devices in bfloat16 or wider.
A program may use at most 1 GiB of HBM per device.

v0:
```python
import math
import jax
import jax.numpy as jnp
from jax import lax
from jax.sharding import PartitionSpec as P, NamedSharding


def dft_block(length):
    positions = jnp.arange(length)
    phase_steps = (positions[:, None] * positions[None, :]) % length
    angles = phase_steps.astype(jnp.float32) * (2.0 * math.pi / length)
    norm_scale = 1.0 / math.sqrt(length)
    cos_part = jnp.cos(angles) * norm_scale
    sin_part = jnp.sin(angles) * norm_scale
    real_rows = jnp.stack([cos_part, sin_part], axis=1)
    imag_rows = jnp.stack([-sin_part, cos_part], axis=1)
    return jnp.stack([real_rows, imag_rows])


def solution(mesh):
    highest = lax.Precision.HIGHEST

    def local_forward(u_real, u_imag, g_filter):
        dft_mat = dft_block(u_real.shape[1])
        field_pair = jnp.stack([u_real, u_imag])
        field_pair = jnp.einsum("dkcx,cbxyz->dbkyz", dft_mat, field_pair, precision=highest, preferred_element_type=jnp.float32)
        field_pair = lax.all_to_all(field_pair, "row", 2, 3, tiled=True)
        field_pair = jnp.einsum("dkcy,cbxyz->dbxkz", dft_mat, field_pair, precision=highest, preferred_element_type=jnp.float32)
        field_pair = lax.all_to_all(field_pair, "col", 3, 4, tiled=True)
        field_pair = jnp.einsum("dkcz,cbxyz->dbxyk", dft_mat, field_pair, precision=highest, preferred_element_type=jnp.float32)
        filtered = field_pair * g_filter
        return filtered[0], filtered[1]

    field_spec = P("fld", None, "row", "col")
    out_spec = P("fld", "row", "col", None)
    return jax.shard_map(local_forward, mesh=mesh, in_specs=(field_spec, field_spec, P("row", "col", None)), out_specs=(out_spec, out_spec), check_vma=False)
```

profile of v0, /device:TPU:0, one launch (start us, length us, event | category | flops | bytes accessed | tf_op | source)
XLA Modules:
  0.0 1636.5 jit_solution(13189873556840340427)
XLA Ops:
  0.6 0.3 fusion.20
  0.9 0.3 sine_multiply_fusion
  1.2 0.0 copy-start
  1.2 0.0 copy-start.3
  1.2 0.6 copy-done
  1.9 0.0 copy-done.3
  1.9 18.6 %fusion.13 = f32[2,16,128,32,32]{2,4,0,3,1:T(8,128)} fusion(f32[1,16,128,32,32]{2,4,0,3,1:T(8,128)} %bitcast.65, f32[1,16,128,32,32]{2,4,0,3,1:T(8,128)} %bitcast.66, f32[1,128,2,128]{3,1,2,0:T(8,128)S(1)} %get-tuple-element.5, f32[1,128,2,128]{3,1,2,0:T(8,128)S(1)} %get-tuple-element.4), kind=kOutput, calls=%fused_computation.12 | convolution fusion | flops 12889161728 | bytes 33816576 | tf_op jit(solution)/shard_map/dkcx,cbxyz->dbkyz/dot_general | solution.py:26
  20.5 79.0 %copy.7 = f32[2,16,128,32,32]{4,0,3,1,2:T(2,128)} copy(f32[2,16,128,32,32]{2,4,0,3,1:T(8,128)} %fusion.13) | data formatting | bytes 33554432 | tf_op jit(solution)/shard_map/dkcx,cbxyz->dbkyz/transpose | solution.py:26
  99.5 108.8 %reshape.95 = f32[4,1,1048576]{2,1,0:T(1,128)} reshape(f32[128,16,32,2,32]{4,3,2,1,0:T(2,128)} %bitcast.60) | data formatting | bytes 33554432
  208.3 194.5 %all_to_all.36 = f32[4,1,1048576]{2,1,0:T(1,128)} all-to-all(f32[4,1,1048576]{2,1,0:T(1,128)} %reshape.95), channel_id=1, replica_groups=mesh['fld'=2,'col'=4,'row'=4] {'row'}, dimensions={0} | all-to-all | bytes 33554432 | tf_op jit(solution)/shard_map/all_to_all | solution.py:27
  402.8 0.5 broadcast.141
  403.3 54.3 %reduce = f32[4,1048576]{1,0:T(4,128)} reduce(f32[4,1,1048576]{2,1,0:T(1,128)} %all_to_all.36, f32[]{:T(128)} %broadcast.141), dimensions={1}, to_apply=%all_to_all.26.reduce_sub_computation | reduce | bytes 33554436 | tf_op jit(solution)/shard_map/all_to_all | solution.py:27
  457.6 124.8 %reshape.96 = f32[128,16,32,2,32]{4,3,2,1,0:T(2,128)} reshape(f32[4,1048576]{1,0:T(4,128)} %reduce) | data formatting | bytes 33554432
  582.4 96.3 %copy.8 = f32[2,16,4,32,32,32]{4,2,5,0,3,1:T(4,128)} copy(f32[2,16,4,32,32,32]{5,0,4,1,3,2:T(2,128)} %bitcast.11) | data formatting | bytes 33554432 | tf_op jit(solution)/shard_map/all_to_all | solution.py:27
  678.7 0.0 copy-start.1
  678.7 0.0 copy-start.4
  678.7 50.2 %reshape.89 = f32[2,16,32,128,32,1]{3,4,0,2,1,5:T(8,128)} reshape(f32[2,16,32,4,32,32]{4,3,5,0,2,1:T(4,128)} %bitcast.12) | data formatting | bytes 33554432 | tf_op jit(solution)/shard_map/all_to_all | solution.py:27
  728.9 0.0 copy-done.1
  728.9 0.0 copy-done.4
  729.0 18.6 %fusion.10 = f32[2,16,32,128,32]{3,4,0,2,1:T(8,128)} fusion(f32[2,16,32,128,32,1]{3,4,0,2,1,5:T(8,128)} %reshape.89, f32[1,128,2,128]{3,1,2,0:T(8,128)S(1)} %copy-done.4, f32[1,128,2,128]{3,1,2,0:T(8,128)S(1)} %copy-done.1), kind=kOutput, calls=%fused_computation.11 | convolution fusion | flops 12884967424 | bytes 33816576 | tf_op jit(solution)/shard_map/dkcy,cbxyz->dbxkz/dot_general | solution.py:28
  747.6 79.0 %copy.9 = f32[2,16,32,128,32]{4,0,2,1,3:T(2,128)} copy(f32[2,16,32,128,32]{3,4,0,2,1:T(8,128)} %fusion.10) | data formatting | bytes 33554432 | tf_op jit(solution)/shard_map/dkcy,cbxyz->dbxkz/transpose | solution.py:28
  826.6 108.7 %reshape.97 = f32[4,1,1048576]{2,1,0:T(1,128)} reshape(f32[128,16,32,2,32]{4,3,2,1,0:T(2,128)} %bitcast.62) | data formatting | bytes 33554432
  935.3 374.4 %all_to_all.37 = f32[4,1,1048576]{2,1,0:T(1,128)} all-to-all(f32[4,1,1048576]{2,1,0:T(1,128)} %reshape.97), channel_id=1, replica_groups=mesh['fld'=2,'col'=4,'row'=4] {'col'}, dimensions={0} | all-to-all | bytes 33554432 | tf_op jit(solution)/shard_map/all_to_all | solution.py:29
  1309.7 54.3 %reduce.1 = f32[4,1048576]{1,0:T(4,128)} reduce(f32[4,1,1048576]{2,1,0:T(1,128)} %all_to_all.37, f32[]{:T(128)} %broadcast.141), dimensions={1}, to_apply=%all_to_all.30.reduce_sub_computation | reduce | bytes 33554436 | tf_op jit(solution)/shard_map/all_to_all | solution.py:29
  1364.0 124.8 %reshape.98 = f32[128,16,32,2,32]{4,3,2,1,0:T(2,128)} reshape(f32[4,1048576]{1,0:T(4,128)} %reduce.1) | data formatting | bytes 33554432
  1488.8 73.1 %copy.19 = f32[2,16,32,4,32,32]{5,3,4,0,2,1:T(4,128)} copy(f32[2,16,32,4,32,32]{5,0,2,1,4,3:T(2,128)} %bitcast.17) | data formatting | bytes 33554432 | tf_op jit(solution)/shard_map/all_to_all | solution.py:29
  1561.9 0.0 copy-start.2
  1561.9 0.0 copy-start.5
  1561.9 0.0 copy-start.6
  1561.9 50.4 %reshape.91 = f32[2,16,32,32,128,1]{4,3,0,2,1,5:T(8,128)} reshape(f32[2,16,32,32,4,32]{5,4,3,0,2,1:T(4,128)} %bitcast.64) | data formatting | bytes 33554432 | tf_op jit(solution)/shard_map/all_to_all | solution.py:29
  1612.3 0.0 copy-done.2
  1612.3 0.0 copy-done.5
  1612.3 0.0 copy-done.6
  1612.3 17.0 %fusion.3 = f32[2,16,32,32,128]{4,3,0,2,1:T(8,128)S(1)} fusion(f32[2,16,32,32,128,1]{4,3,0,2,1,5:T(8,128)} %reshape.91, f32[32,32,128]{2,1,0:T(8,128)S(1)} %copy-done.6, f32[1,128,2,128]{3,1,2,0:T(8,128)S(1)} %copy-done.5, f32[1,128,2,128]{3,1,2,0:T(8,128)S(1)} %copy-done.2), kind=kOutput, calls=%fused_computation.6 | convolution fusion | flops 12889161728 | bytes 34340864 | tf_op jit(solution)/shard_map/dkcz,cbxyz->dbxyk/dot_general | solution.py:30
  1629.3 7.0 slice_bitcast_fusion
  (1 shorter events, 0.0 us)
Async XLA Ops:
  1.2 0.7 copy-start
  1.2 0.7 copy-start.3
  678.7 50.2 %copy-start.1 = (f32[1,128,2,128]{3,1,2,0:T(8,128)S(1)}, f32[1,128,2,128]{3,1,2,0:T(8,128)}, u32[]{:S(2)}) copy-start(f32[1,128,2,128]{3,1,2,0:T(8,128)} %copy-done) | copy-start | bytes 393220
  678.7 50.2 %copy-start.4 = (f32[1,128,2,128]{3,1,2,0:T(8,128)S(1)}, f32[1,128,2,128]{3,1,2,0:T(8,128)}, u32[]{:S(2)}) copy-start(f32[1,128,2,128]{3,1,2,0:T(8,128)} %copy-done.3) | copy-start | bytes 393220
  1561.9 50.4 %copy-start.2 = (f32[1,128,2,128]{3,1,2,0:T(8,128)S(1)}, f32[1,128,2,128]{3,1,2,0:T(8,128)}, u32[]{:S(2)}) copy-start(f32[1,128,2,128]{3,1,2,0:T(8,128)} %copy-done) | copy-start | bytes 393220
  1561.9 50.4 %copy-start.5 = (f32[1,128,2,128]{3,1,2,0:T(8,128)S(1)}, f32[1,128,2,128]{3,1,2,0:T(8,128)}, u32[]{:S(2)}) copy-start(f32[1,128,2,128]{3,1,2,0:T(8,128)} %copy-done.3) | copy-start | bytes 393220
  1561.9 50.4 %copy-start.6 = (f32[32,32,128]{2,1,0:T(8,128)S(1)}, f32[32,32,128]{2,1,0:T(8,128)}, u32[]{:S(2)}) copy-start(f32[32,32,128]{2,1,0:T(8,128)} %param.5) | copy-start | bytes 1572868
where the time goes:
time: 1650 us; the launch traced here: 1640 us
  local copies, waits for them, and re-layouts  903 us (55%)
  blocking collectives  569 us (34%)
  other arithmetic  109 us (7%)
  matrix products  54.2 us (3%)
    unnamed x18, local copies, waits for them, and re-layouts  468 us
    all_to_all x1, blocking collectives, local_forward(): field_pair = lax.all_to_all(field_pair, 'col', 3, 4, tiled=True)  374 us
    all_to_all x1, blocking collectives, local_forward(): field_pair = lax.all_to_all(field_pair, 'row', 2, 3, tiled=True)  194 us
    all_to_all x3, local copies, waits for them, and re-layouts, local_forward(): field_pair = lax.all_to_all(field_pair, 'row', 2, 3, tiled=True)  147 us
    all_to_all x2, local copies, waits for them, and re-layouts, local_forward(): field_pair = lax.all_to_all(field_pair, 'col', 3, 4, tiled=True)  123 us
    transpose x1, local copies, waits for them, and re-layouts, local_forward(): jnp.einsum('dkcx,cbxyz->dbkyz', dft_mat, field_pair, precision=highest, p...  79 us
    transpose x1, local copies, waits for them, and re-layouts, local_forward(): jnp.einsum('dkcy,cbxyz->dbxkz', dft_mat, field_pair, precision=highest, p...  79 us
    all_to_all x1, other arithmetic, local_forward(): field_pair = lax.all_to_all(field_pair, 'col', 3, 4, tiled=True)  54.3 us

commit v1 on v0

v1 whole, which is shorter than its diff:
```python
import functools
import math

import jax
import jax.numpy as jnp
import numpy as np
from jax import lax
from jax.experimental import pallas as pl
from jax.experimental.pallas import tpu as pltpu
from jax.sharding import PartitionSpec as P

MESH = pl.DeviceIdType.MESH
N = 128
B = 32
NP = 4
FG = 4
KC = 8
NJ = B // KC
MSG = 2 * KC * B
SC = 16
TINY = 2.0 ** -126


def dft_tables():
    idx = np.arange(N)
    ang = 2.0 * np.pi * ((idx[:, None] * idx[None, :]) % N) / N
    cos, sin = np.cos(ang) / math.sqrt(N), np.sin(ang) / math.sqrt(N)
    mat = np.stack([np.stack([cos, sin], 1), np.stack([-sin, cos], 1)])
    fx = mat.reshape(2, NP, NJ, KC, 2 * N).transpose(1, 2, 0, 3, 4).reshape(2 * N, 2 * N)
    fy = mat.reshape(2, NP, B, 2, NP, B).transpose(1, 0, 2, 4, 3, 5).reshape(2 * N, 2 * N)
    fz = mat.transpose(2, 3, 0, 1).reshape(2 * N, 2 * N)
    return fx.astype(np.float32), fy.astype(np.float32), fz.astype(np.float32)


def encode(x, scale):
    v = x * (1.0 / scale)
    p = v * v
    p = p * p
    p = p * p
    return jnp.where(v < 0, -p, p).astype(jnp.bfloat16)


def decode(code, scale):
    y = code.astype(jnp.float32)
    p = jnp.maximum(jnp.abs(y), TINY)
    root = lax.rsqrt(lax.rsqrt(p * lax.rsqrt(p)))
    return jnp.where(y < 0, -root, root) * scale


def scale_of(peak):
    return jnp.maximum(peak * 2.0 ** -15, TINY).astype(jnp.bfloat16).astype(jnp.float32)


def kernel(ng, fx_ref, fy_ref, fz_ref, g_ref, ur_ref, ui_ref, wr_ref, wi_ref,
           stage, xsend, xrecv, ysend, yrecv, scales, ostage,
           in_sem, xs_sem, xr_sem, ys_sem, yr_sem, out_sem):
    nt = ng * NJ
    col, row = lax.axis_index("col"), lax.axis_index("row")
    highest = lax.Precision.HIGHEST

    def peer(me, d):
        return lax.rem(me + d, NP)

    def load(grp, slot):
        copies = []
        for c, src in enumerate((ur_ref, ui_ref)):
            copies.append(pltpu.make_async_copy(src.at[pl.ds(grp * FG, FG)], stage.at[slot, c], in_sem.at[slot, c]))
        return copies

    def row_copy(t, d):
        dst = peer(row, d)
        base = pl.multiple_of((lax.rem(t, 2 * NJ) // NJ * NP * NJ + dst * NJ + lax.rem(t, NJ)) * MSG, MSG)
        src = xsend.at[pl.ds(base, MSG)]
        if d == 0:
            return pltpu.make_async_copy(src, xrecv.at[t, row], xr_sem.at[t, row])
        return pltpu.make_async_remote_copy(
            src, xrecv.at[t, row], xs_sem.at[lax.rem(t, 2 * NJ), d], xr_sem.at[t, row],
            device_id={"row": dst}, device_id_type=MESH)

    def col_copy(t, d):
        dst = peer(col, d)
        src = ysend.at[lax.rem(t, 4), dst]
        if d == 0:
            return pltpu.make_async_copy(src, yrecv.at[t, col], yr_sem.at[t, col])
        return pltpu.make_async_remote_copy(
            src, yrecv.at[t, col], ys_sem.at[lax.rem(t, 4), d], yr_sem.at[t, col],
            device_id={"col": dst}, device_id_type=MESH)

    def arrived(buf, sem, t):
        for p in range(NP):
            pltpu.make_async_copy(buf.at[t, p], buf.at[t, p], sem.at[t, p]).wait()

    def x_step(grp):
        slot = lax.rem(grp, 2)
        for copy in load(grp, slot):
            copy.wait()

        def body(yy, _):
            pieces = []
            for dy in range(2):
                y = yy * 2 + dy
                halves = [stage[slot, c, :, pl.ds(y, 1)].reshape(FG * B, N) for c in range(2)]
                pieces.append(jnp.concatenate(halves, axis=1))
            data = jnp.concatenate(pieces, axis=0)
            out = lax.dot_general(fx_ref[...], data, (((1,), (1,)), ((), ())), precision=highest,
                                  preferred_element_type=jnp.float32)
            for dy in range(2):
                for blk in range(2 * NP * NJ):
                    base = slot * (NP * NJ * MSG) + (blk // 2) * MSG + (blk % 2) * B + yy * 2 + dy
                    xsend[pl.ds(base, KC, stride=2 * B), :] = out[blk * KC:(blk + 1) * KC, dy * N:(dy + 1) * N]
            return 0

        lax.fori_loop(0, B // 2, body, 0)

        def send(j, _):
            for d in (2, 1, 3, 0):
                row_copy(grp * NJ + j, d).start()
            return 0

        lax.fori_loop(0, NJ, send, 0)

    def row_drained(grp):
        def body(j, _):
            for d in (1, 2, 3):
                row_copy(grp * NJ + j, d).wait_send()
            return 0

        lax.fori_loop(0, NJ, body, 0)

    def y_step(t):
        slot = lax.rem(t, 4)
        arrived(xrecv, xr_sem, t)

        def body(kk, _):
            cols = []
            for dk in range(2):
                k = kk * 2 + dk
                rows = pl.ds(pl.multiple_of(k * 2 * B, 2 * B), 2 * B)
                cols.append(jnp.concatenate([xrecv[t, p, rows, :] for p in range(NP)], axis=0))
            data = jnp.concatenate(cols, axis=1)
            out = jnp.dot(fy_ref[...], data, precision=highest, preferred_element_type=jnp.float32)
            scale = scale_of(jnp.max(jnp.abs(out), axis=0, keepdims=True))
            out = encode(out, scale)
            for dk in range(2):
                scales[pl.ds(kk * 2 + dk, 1), :] = scale[:, dk * N:(dk + 1) * N]
                for s in range(NP):
                    for c in range(2):
                        rows = pl.ds(pl.multiple_of(c * KC * B + (kk * 2 + dk) * B, B), B)
                        ysend[slot, s, rows, :] = out[(s * 2 + c) * B:(s * 2 + c + 1) * B, dk * N:(dk + 1) * N]
            return 0

        lax.fori_loop(0, KC // 2, body, 0)
        tail = jnp.concatenate([scales[...]] * (SC // KC), axis=0).astype(jnp.bfloat16)
        for s in range(NP):
            ysend[slot, s, MSG:MSG + SC, :] = tail
        for d in (2, 3, 1, 0):
            col_copy(t, d).start()

    def out_copies(t):
        slot = lax.rem(t, 2)
        grp, j = t // NJ, lax.rem(t, NJ)
        return [pltpu.make_async_copy(
            ostage.at[slot, c], dst.at[pl.ds(grp * FG, FG), pl.ds(j * KC, KC)], out_sem.at[slot, c])
            for c, dst in enumerate((wr_ref, wi_ref))]

    def z_step(t):
        slot, j = lax.rem(t, 2), lax.rem(t, NJ)
        arrived(yrecv, yr_sem, t)
        half = KC * B
        gain = g_ref[pl.ds(j * KC, KC)].reshape(half, N)
        group = lax.broadcasted_iota(jnp.int32, (MSG + SC, N), 1) // B
        for f in range(FG):
            code = None
            for q in range(NP):
                piece = yrecv[t, q]
                if q != f:
                    piece = pltpu.roll(piece, (q - f) % NP * B, 1)
                code = piece if code is None else jnp.where(group == q, piece, code)
            rows = code[MSG:].astype(jnp.float32)
            scale = jnp.concatenate([jnp.broadcast_to(rows[k:k + 1], (B, N)) for k in range(KC)], axis=0)
            data = jnp.concatenate([decode(code[c * half:(c + 1) * half], scale) for c in range(2)], axis=1)
            out = jnp.dot(data, fz_ref[...], precision=highest, preferred_element_type=jnp.float32)
            for c in range(2):
                ostage[slot, c, f] = (out[:, c * N:(c + 1) * N] * gain).reshape(KC, B, N)
        for copy in out_copies(t):
            copy.start()

    for grp in range(min(2, ng)):
        for copy in load(grp, grp):
            copy.start()

    barrier = pltpu.get_barrier_semaphore()
    for d in range(1, NP):
        pl.semaphore_signal(barrier, inc=1, device_id={"row": peer(row, d)}, device_id_type=MESH)
        pl.semaphore_signal(barrier, inc=1, device_id={"col": peer(col, d)}, device_id_type=MESH)
    pl.semaphore_wait(barrier, 2 * (NP - 1))

    x_step(0)

    if ng > 1:
        x_step(1)
    if ng > 2:
        for copy in load(2, 0):
            copy.start()

    def tick(t, _):
        @pl.when(t >= 4)
        def _():
            for d in (1, 2, 3):
                col_copy(t - 4, d).wait_send()

        y_step(t)

        @pl.when(t >= 1)
        def _():
            @pl.when(t >= 3)
            def _():
                for copy in out_copies(t - 3):
                    copy.wait()

            z_step(t - 1)

        if ng > 2:
            @pl.when((lax.rem(t, NJ) == NJ - 1) & (t < (ng - 2) * NJ))
            def _():
                grp = t // NJ
                row_drained(grp)
                x_step(grp + 2)

                @pl.when(grp + 3 < ng)
                def _():
                    for copy in load(grp + 3, lax.rem(grp + 3, 2)):
                        copy.start()

        return 0

    lax.fori_loop(0, nt, tick, 0)

    for copy in out_copies(nt - 3):
        copy.wait()
    z_step(nt - 1)
    for t in (nt - 2, nt - 1):
        for copy in out_copies(t):
            copy.wait()
    for grp in range(max(ng - 2, 0), ng):
        row_drained(grp)
    for t in range(nt - 4, nt):
        for d in (1, 2, 3):
            col_copy(t, d).wait_send()


def solution(mesh):
    fx, fy, fz = dft_tables()

    def local_forward(u_real, u_imag, g_filter):
        ng = u_real.shape[0] // FG
        nt = ng * NJ
        u_real, u_imag = (jnp.transpose(u, (0, 2, 3, 1)) for u in (u_real, u_imag))
        out = jax.ShapeDtypeStruct((ng * FG, B, B, N), jnp.float32)
        vmem, anywhere = pl.BlockSpec(memory_space=pltpu.VMEM), pl.BlockSpec(memory_space=pl.ANY)
        flops = 2 * 2 * N * 2 * N * N * B * B // N * ng * FG * 24
        return pl.pallas_call(
            functools.partial(kernel, ng),
            out_shape=(out, out),
            in_specs=[vmem] * 4 + [anywhere] * 2,
            out_specs=(anywhere, anywhere),
            scratch_shapes=[
                pltpu.VMEM((2, 2, FG, B, B, N), jnp.float32),
                pltpu.VMEM((2 * NP * NJ * MSG, N), jnp.float32),
                pltpu.VMEM((nt, NP, MSG, N), jnp.float32),
                pltpu.VMEM((4, NP, MSG + SC, N), jnp.bfloat16),
                pltpu.VMEM((nt, NP, MSG + SC, N), jnp.bfloat16),
                pltpu.VMEM((KC, N), jnp.float32),
                pltpu.VMEM((2, 2, FG, KC, B, N), jnp.float32),
                pltpu.SemaphoreType.DMA((2, 2)),
                pltpu.SemaphoreType.DMA((2 * NJ, NP)),
                pltpu.SemaphoreType.DMA((nt, NP)),
                pltpu.SemaphoreType.DMA((4, NP)),
                pltpu.SemaphoreType.DMA((nt, NP)),
                pltpu.SemaphoreType.DMA((2, 2)),
            ],
            compiler_params=pltpu.CompilerParams(
                collective_id=0, has_side_effects=True, vmem_limit_bytes=67043328),
            cost_estimate=pl.CostEstimate(flops=flops, bytes_accessed=1 << 25, transcendentals=0),
        )(jnp.asarray(fx), jnp.asarray(fy), jnp.asarray(fz), g_filter, u_real, u_imag)

    field_spec = P("fld", None, "row", "col")
    out_spec = P("fld", "row", "col", None)
    return jax.shard_map(local_forward, mesh=mesh, in_specs=(field_spec, field_spec, P("row", "col", None)),
                         out_specs=(out_spec, out_spec), check_vma=False)
```

time: 1650 us -> 239 us (0.14)
  local copies, waits for them, and re-layouts: 903 us -> 11.7 us
  blocking collectives: 569 us -> 0 us
  Pallas kernels: 0 us -> 226 us
  other arithmetic: 109 us -> 0 us
  matrix products: 54.2 us -> 0 us
    all_to_all x2 -> x0, blocking collectives: 569 us -> none  [the longest x1 374 us: local_forward(): field_pair = lax.all_to_all(field_pair, 'col', 3, 4, tiled=True)]
    unnamed x18 -> x4, local copies, waits for them, and re-layouts: 468 us -> 11.7 us
    all_to_all x5 -> x0, local copies, waits for them, and re-layouts: 271 us -> none  [the longest x3 147 us: local_forward(): field_pair = lax.all_to_all(field_pair, 'row', 2, 3, tiled=True)]
    pallas_call x0 -> x1, Pallas kernels: none -> 226 us  [local_forward(): pl.pallas_call(functools.partial(kernel, ng), out_shape=(out, out), in_sp...]
    transpose x2 -> x0, local copies, waits for them, and re-layouts: 158 us -> none  [the longest x1 79 us: local_forward(): jnp.einsum('dkcx,cbxyz->dbkyz', dft_mat, field_pair, precision=highest, p...]
    all_to_all x2 -> x0, other arithmetic: 109 us -> none  [the longest x1 54.3 us: local_forward(): field_pair = lax.all_to_all(field_pair, 'col', 3, 4, tiled=True)]
    dot_general x3 -> x0, matrix products: 54.2 us -> none  [the longest x1 18.6 us: local_forward(): jnp.einsum('dkcy,cbxyz->dbxkz', dft_mat, field_pair, precision=highest, p...]
where the time goes in v1:
time: 239 us
  Pallas kernels  226 us (95%)
  local copies, waits for them, and re-layouts  11.7 us (5%)
    pallas_call x1, Pallas kernels, local_forward(): pl.pallas_call(functools.partial(kernel, ng), out_shape=(out, out), in_sp...  226 us
    unnamed x4, local copies, waits for them, and re-layouts  11.7 us

profile of v1, /device:TPU:0, one launch (start us, length us, event | category | flops | bytes accessed | tf_op | source)
XLA Modules:
  0.0 238.7 jit_solution(4738322735495434051)
XLA Ops:
  0.6 226.4 %shard_map.77 = (f32[16,32,32,128]{3,2,1,0:T(8,128)}, f32[16,32,32,128]{3,2,1,0:T(8,128)}) custom-call(f32[256,256]{1,0:T(8,128)} %constant.6.clone.fx_ref, f32[256,256]{1,0:T(8,128)} %constant.7.clone.fy_ref, f32[256,256]{1,0:T(8,128)} %constant.8.clone.fz_ref, f32[32,32,128]{2,1,0:T(8,128)} %g_ref.1, f32[16,32,32,128]{3,2,1,0:T(8,128)} %bitcast.2, ...), custom_call_target="tpu_custom_call" | custom-call | flops 51539607552 | bytes 33554432 | tf_op jit(solution)/shard_map/pallas_call | solution.py:262
  227.0 0.0 copy-start
  227.0 8.3 %copy.10 = f32[16,32,32,128]{3,2,1,0:T(8,128)} copy(f32[16,32,32,128]{3,2,1,0:T(8,128)} %get-tuple-element.4) | data formatting | bytes 16777216
  235.3 0.0 copy-done
  235.3 3.4 %copy.11 = f32[16,32,32,128]{3,2,1,0:T(8,128)} copy(f32[16,32,32,128]{3,2,1,0:T(8,128)S(1)} %copy-done) | data formatting | bytes 16777216
Async XLA Ops:
  227.0 8.3 %copy-start = (f32[16,32,32,128]{3,2,1,0:T(8,128)S(1)}, f32[16,32,32,128]{3,2,1,0:T(8,128)}, u32[]{:S(2)}) copy-start(f32[16,32,32,128]{3,2,1,0:T(8,128)} %get-tuple-element.5) | copy-start | bytes 25165828

commit v2 on v1

--- a/solution.py
+++ b/solution.py
@@ -52,8 +52,8 @@
 
 
 def kernel(ng, fx_ref, fy_ref, fz_ref, g_ref, ur_ref, ui_ref, wr_ref, wi_ref,
-           stage, xsend, xrecv, ysend, yrecv, scales, ostage,
-           in_sem, xs_sem, xr_sem, ys_sem, yr_sem, out_sem):
+           stage, xout, xsend, xrecv, ysend, yrecv, scales,
+           in_sem, xs_sem, xr_sem, ys_sem, yr_sem):
     nt = ng * NJ
     col, row = lax.axis_index("col"), lax.axis_index("row")
     highest = lax.Precision.HIGHEST
@@ -69,8 +69,7 @@
 
     def row_copy(t, d):
         dst = peer(row, d)
-        base = pl.multiple_of((lax.rem(t, 2 * NJ) // NJ * NP * NJ + dst * NJ + lax.rem(t, NJ)) * MSG, MSG)
-        src = xsend.at[pl.ds(base, MSG)]
+        src = xsend.at[lax.rem(t, 2 * NJ), dst]
         if d == 0:
             return pltpu.make_async_copy(src, xrecv.at[t, row], xr_sem.at[t, row])
         return pltpu.make_async_remote_copy(
@@ -95,7 +94,7 @@
         for copy in load(grp, slot):
             copy.wait()
 
-        def body(yy, _):
+        def body(yy, peak):
             pieces = []
             for dy in range(2):
                 y = yy * 2 + dy
@@ -106,15 +105,28 @@
                                   preferred_element_type=jnp.float32)
             for dy in range(2):
                 for blk in range(2 * NP * NJ):
-                    base = slot * (NP * NJ * MSG) + (blk // 2) * MSG + (blk % 2) * B + yy * 2 + dy
-                    xsend[pl.ds(base, KC, stride=2 * B), :] = out[blk * KC:(blk + 1) * KC, dy * N:(dy + 1) * N]
-            return 0
-
-        lax.fori_loop(0, B // 2, body, 0)
+                    base = blk // 2 * MSG + blk % 2 * B + yy * 2 + dy
+                    xout[pl.ds(base, KC, stride=2 * B), :] = out[blk * KC:(blk + 1) * KC, dy * N:(dy + 1) * N]
+            tall = jnp.max(jnp.abs(out).reshape(2 * N // 8, 8, 2 * N), axis=0)
+            return jnp.maximum(peak, jnp.maximum(tall[:, :N], tall[:, N:]))
+
+        peak = lax.fori_loop(0, B // 2, body, jnp.zeros((8, N), jnp.float32))
+        scale = scale_of(jnp.max(peak, axis=0, keepdims=True))
+        tail = jnp.broadcast_to(scale, (SC, N)).astype(jnp.bfloat16)
 
         def send(j, _):
+            t = grp * NJ + j
+            place = lax.rem(t, 2 * NJ)
+
+            def pack(r, _):
+                rows = pl.ds(pl.multiple_of((r * NJ + j) * MSG, MSG), MSG)
+                xsend[place, r, :MSG, :] = encode(xout[rows, :], scale)
+                xsend[place, r, MSG:, :] = tail
+                return 0
+
+            lax.fori_loop(0, NP, pack, 0)
             for d in (2, 1, 3, 0):
-                row_copy(grp * NJ + j, d).start()
+                row_copy(t, d).start()
             return 0
 
         lax.fori_loop(0, NJ, send, 0)
@@ -136,7 +148,9 @@
             for dk in range(2):
                 k = kk * 2 + dk
                 rows = pl.ds(pl.multiple_of(k * 2 * B, 2 * B), 2 * B)
-                cols.append(jnp.concatenate([xrecv[t, p, rows, :] for p in range(NP)], axis=0))
+                cols.append(jnp.concatenate(
+                    [decode(xrecv[t, p, rows, :], xrecv[t, p, MSG:, :].astype(jnp.float32)[:1]) for p in range(NP)],
+                    axis=0))
             data = jnp.concatenate(cols, axis=1)
             out = jnp.dot(fy_ref[...], data, precision=highest, preferred_element_type=jnp.float32)
             scale = scale_of(jnp.max(jnp.abs(out), axis=0, keepdims=True))
@@ -156,15 +170,8 @@
         for d in (2, 3, 1, 0):
             col_copy(t, d).start()
 
-    def out_copies(t):
-        slot = lax.rem(t, 2)
+    def z_step(t):
         grp, j = t // NJ, lax.rem(t, NJ)
-        return [pltpu.make_async_copy(
-            ostage.at[slot, c], dst.at[pl.ds(grp * FG, FG), pl.ds(j * KC, KC)], out_sem.at[slot, c])
-            for c, dst in enumerate((wr_ref, wi_ref))]
-
-    def z_step(t):
-        slot, j = lax.rem(t, 2), lax.rem(t, NJ)
         arrived(yrecv, yr_sem, t)
         half = KC * B
         gain = g_ref[pl.ds(j * KC, KC)].reshape(half, N)
@@ -180,10 +187,8 @@
             scale = jnp.concatenate([jnp.broadcast_to(rows[k:k + 1], (B, N)) for k in range(KC)], axis=0)
             data = jnp.concatenate([decode(code[c * half:(c + 1) * half], scale) for c in range(2)], axis=1)
             out = jnp.dot(data, fz_ref[...], precision=highest, preferred_element_type=jnp.float32)
-            for c in range(2):
-                ostage[slot, c, f] = (out[:, c * N:(c + 1) * N] * gain).reshape(KC, B, N)
-        for copy in out_copies(t):
-            copy.start()
+            for c, dst in enumerate((wr_ref, wi_ref)):
+                dst[grp * FG + f, pl.ds(j * KC, KC)] = (out[:, c * N:(c + 1) * N] * gain).reshape(KC, B, N)
 
     for grp in range(min(2, ng)):
         for copy in load(grp, grp):
@@ -213,11 +218,6 @@
 
         @pl.when(t >= 1)
         def _():
-            @pl.when(t >= 3)
-            def _():
-                for copy in out_copies(t - 3):
-                    copy.wait()
-
             z_step(t - 1)
 
         if ng > 2:
@@ -236,12 +236,7 @@
 
     lax.fori_loop(0, nt, tick, 0)
 
-    for copy in out_copies(nt - 3):
-        copy.wait()
     z_step(nt - 1)
-    for t in (nt - 2, nt - 1):
-        for copy in out_copies(t):
-            copy.wait()
     for grp in range(max(ng - 2, 0), ng):
         row_drained(grp)
     for t in range(nt - 4, nt):
@@ -256,31 +251,30 @@
         ng = u_real.shape[0] // FG
         nt = ng * NJ
         u_real, u_imag = (jnp.transpose(u, (0, 2, 3, 1)) for u in (u_real, u_imag))
-        out = jax.ShapeDtypeStruct((ng * FG, B, B, N), jnp.float32)
+        out = pltpu.VMEM((ng * FG, B, B, N), jnp.float32)
         vmem, anywhere = pl.BlockSpec(memory_space=pltpu.VMEM), pl.BlockSpec(memory_space=pl.ANY)
         flops = 2 * 2 * N * 2 * N * N * B * B // N * ng * FG * 24
         return pl.pallas_call(
             functools.partial(kernel, ng),
             out_shape=(out, out),
             in_specs=[vmem] * 4 + [anywhere] * 2,
-            out_specs=(anywhere, anywhere),
+            out_specs=(vmem, vmem),
             scratch_shapes=[
                 pltpu.VMEM((2, 2, FG, B, B, N), jnp.float32),
-                pltpu.VMEM((2 * NP * NJ * MSG, N), jnp.float32),
-                pltpu.VMEM((nt, NP, MSG, N), jnp.float32),
+                pltpu.VMEM((NP * NJ * MSG, N), jnp.float32),
+                pltpu.VMEM((2 * NJ, NP, MSG + SC, N), jnp.bfloat16),
+                pltpu.VMEM((nt, NP, MSG + SC, N), jnp.bfloat16),
                 pltpu.VMEM((4, NP, MSG + SC, N), jnp.bfloat16),
                 pltpu.VMEM((nt, NP, MSG + SC, N), jnp.bfloat16),
                 pltpu.VMEM((KC, N), jnp.float32),
-                pltpu.VMEM((2, 2, FG, KC, B, N), jnp.float32),
                 pltpu.SemaphoreType.DMA((2, 2)),
                 pltpu.SemaphoreType.DMA((2 * NJ, NP)),
                 pltpu.SemaphoreType.DMA((nt, NP)),
                 pltpu.SemaphoreType.DMA((4, NP)),
                 pltpu.SemaphoreType.DMA((nt, NP)),
-                pltpu.SemaphoreType.DMA((2, 2)),
             ],
             compiler_params=pltpu.CompilerParams(
-                collective_id=0, has_side_effects=True, vmem_limit_bytes=67043328),
+                collective_id=0, has_side_effects=True, vmem_limit_bytes=40 << 20),
             cost_estimate=pl.CostEstimate(flops=flops, bytes_accessed=1 << 25, transcendentals=0),
         )(jnp.asarray(fx), jnp.asarray(fy), jnp.asarray(fz), g_filter, u_real, u_imag)
 

time: 239 us -> 241 us (level)
  Pallas kernels: 226 us -> 234 us
  local copies, waits for them, and re-layouts: 11.7 us -> 6.8 us
    pallas_call x1, Pallas kernels: 226 us -> 234 us  [local_forward(): pl.pallas_call(functools.partial(kernel, ng), out_shape=(out, out), in_sp...]
    unnamed x4 -> x2, local copies, waits for them, and re-layouts: 11.7 us -> 6.8 us
where the time goes in v2:
time: 241 us
  Pallas kernels  234 us (97%)
  local copies, waits for them, and re-layouts  6.8 us (3%)
    pallas_call x1, Pallas kernels, local_forward(): pl.pallas_call(functools.partial(kernel, ng), out_shape=(out, out), in_sp...  234 us
    unnamed x2, local copies, waits for them, and re-layouts  6.8 us

profile of v2, /device:TPU:0, one launch (start us, length us, event | category | flops | bytes accessed | tf_op | source)
XLA Modules:
  0.0 241.1 jit_solution(6585853620568020593)
XLA Ops:
  0.6 233.7 %shard_map.77 = (f32[16,32,32,128]{3,2,1,0:T(8,128)S(1)}, f32[16,32,32,128]{3,2,1,0:T(8,128)S(1)}) custom-call(f32[256,256]{1,0:T(8,128)} %constant.6.clone.fx_ref, f32[256,256]{1,0:T(8,128)} %constant.7.clone.fy_ref, f32[256,256]{1,0:T(8,128)} %constant.8.clone.fz_ref, f32[32,32,128]{2,1,0:T(8,128)} %g_ref.1, f32[16,32,32,128]{3,2,1,0:T(8,128)} %bitcast.2, ...), custom_call_target="tpu_custom_call" | custom-call | flops 51539607552 | bytes 33554432 | tf_op jit(solution)/shard_map/pallas_call | solution.py:257
  234.3 3.4 %copy.10 = f32[16,32,32,128]{3,2,1,0:T(8,128)} copy(f32[16,32,32,128]{3,2,1,0:T(8,128)S(1)} %get-tuple-element.2) | data formatting | bytes 16777216
  237.7 3.4 %copy.11 = f32[16,32,32,128]{3,2,1,0:T(8,128)} copy(f32[16,32,32,128]{3,2,1,0:T(8,128)S(1)} %get-tuple-element.3) | data formatting | bytes 16777216

commit v3 on v2

--- a/solution.py
+++ b/solution.py
@@ -19,6 +19,8 @@
 MSG = 2 * KC * B
 SC = 16
 TINY = 2.0 ** -126
+LAG = 6
+YS = LAG + 2
 
 
 def dft_tables():
@@ -59,7 +61,7 @@
     highest = lax.Precision.HIGHEST
 
     def peer(me, d):
-        return lax.rem(me + d, NP)
+        return (me, me + 1 - 2 * lax.rem(me, 2), lax.rem(me + 2, NP), NP - 1 - me)[d]
 
     def load(grp, slot):
         copies = []
@@ -78,11 +80,11 @@
 
     def col_copy(t, d):
         dst = peer(col, d)
-        src = ysend.at[lax.rem(t, 4), dst]
+        src = ysend.at[lax.rem(t, YS), dst]
         if d == 0:
             return pltpu.make_async_copy(src, yrecv.at[t, col], yr_sem.at[t, col])
         return pltpu.make_async_remote_copy(
-            src, yrecv.at[t, col], ys_sem.at[lax.rem(t, 4), d], yr_sem.at[t, col],
+            src, yrecv.at[t, col], ys_sem.at[lax.rem(t, YS), d], yr_sem.at[t, col],
             device_id={"col": dst}, device_id_type=MESH)
 
     def arrived(buf, sem, t):
@@ -125,7 +127,7 @@
                 return 0
 
             lax.fori_loop(0, NP, pack, 0)
-            for d in (2, 1, 3, 0):
+            for d in (2, 3, 1, 0):
                 row_copy(t, d).start()
             return 0
 
@@ -140,7 +142,7 @@
         lax.fori_loop(0, NJ, body, 0)
 
     def y_step(t):
-        slot = lax.rem(t, 4)
+        slot = lax.rem(t, YS)
         arrived(xrecv, xr_sem, t)
 
         def body(kk, _):
@@ -209,16 +211,16 @@
             copy.start()
 
     def tick(t, _):
-        @pl.when(t >= 4)
+        @pl.when(t >= YS)
         def _():
             for d in (1, 2, 3):
-                col_copy(t - 4, d).wait_send()
+                col_copy(t - YS, d).wait_send()
 
         y_step(t)
 
-        @pl.when(t >= 1)
+        @pl.when(t >= LAG)
         def _():
-            z_step(t - 1)
+            z_step(t - LAG)
 
         if ng > 2:
             @pl.when((lax.rem(t, NJ) == NJ - 1) & (t < (ng - 2) * NJ))
@@ -236,10 +238,14 @@
 
     lax.fori_loop(0, nt, tick, 0)
 
-    z_step(nt - 1)
+    def drain(t, _):
+        z_step(t)
+        return 0
+
+    lax.fori_loop(max(nt - LAG, 0), nt, drain, 0)
     for grp in range(max(ng - 2, 0), ng):
         row_drained(grp)
-    for t in range(nt - 4, nt):
+    for t in range(max(nt - YS, 0), nt):
         for d in (1, 2, 3):
             col_copy(t, d).wait_send()
 
@@ -264,17 +270,17 @@
                 pltpu.VMEM((NP * NJ * MSG, N), jnp.float32),
                 pltpu.VMEM((2 * NJ, NP, MSG + SC, N), jnp.bfloat16),
                 pltpu.VMEM((nt, NP, MSG + SC, N), jnp.bfloat16),
-                pltpu.VMEM((4, NP, MSG + SC, N), jnp.bfloat16),
+                pltpu.VMEM((YS, NP, MSG + SC, N), jnp.bfloat16),
                 pltpu.VMEM((nt, NP, MSG + SC, N), jnp.bfloat16),
                 pltpu.VMEM((KC, N), jnp.float32),
                 pltpu.SemaphoreType.DMA((2, 2)),
                 pltpu.SemaphoreType.DMA((2 * NJ, NP)),
                 pltpu.SemaphoreType.DMA((nt, NP)),
-                pltpu.SemaphoreType.DMA((4, NP)),
+                pltpu.SemaphoreType.DMA((YS, NP)),
                 pltpu.SemaphoreType.DMA((nt, NP)),
             ],
             compiler_params=pltpu.CompilerParams(
-                collective_id=0, has_side_effects=True, vmem_limit_bytes=40 << 20),
+                collective_id=0, has_side_effects=True, vmem_limit_bytes=44 << 20),
             cost_estimate=pl.CostEstimate(flops=flops, bytes_accessed=1 << 25, transcendentals=0),
         )(jnp.asarray(fx), jnp.asarray(fy), jnp.asarray(fz), g_filter, u_real, u_imag)
 

time: 241 us -> 227 us (0.942)
  Pallas kernels: 234 us -> 219 us
    pallas_call x1, Pallas kernels: 234 us -> 219 us  [local_forward(): pl.pallas_call(functools.partial(kernel, ng), out_shape=(out, out), in_sp...]
where the time goes in v3:
time: 227 us
  Pallas kernels  219 us (96%)
  local copies, waits for them, and re-layouts  6.8 us (3%)
    pallas_call x1, Pallas kernels, local_forward(): pl.pallas_call(functools.partial(kernel, ng), out_shape=(out, out), in_sp...  219 us
    unnamed x2, local copies, waits for them, and re-layouts  6.8 us

profile of v3, /device:TPU:0, one launch (start us, length us, event | category | flops | bytes accessed | tf_op | source)
XLA Modules:
  0.0 226.6 jit_solution(8559823698302243997)
XLA Ops:
  0.6 219.2 %shard_map.77 = (f32[16,32,32,128]{3,2,1,0:T(8,128)S(1)}, f32[16,32,32,128]{3,2,1,0:T(8,128)S(1)}) custom-call(f32[256,256]{1,0:T(8,128)} %constant.6.clone.fx_ref, f32[256,256]{1,0:T(8,128)} %constant.7.clone.fy_ref, f32[256,256]{1,0:T(8,128)} %constant.8.clone.fz_ref, f32[32,32,128]{2,1,0:T(8,128)} %g_ref.1, f32[16,32,32,128]{3,2,1,0:T(8,128)} %bitcast.2, ...), custom_call_target="tpu_custom_call" | custom-call | flops 51539607552 | bytes 33554432 | tf_op jit(solution)/shard_map/pallas_call | solution.py:263
  219.8 3.4 %copy.10 = f32[16,32,32,128]{3,2,1,0:T(8,128)} copy(f32[16,32,32,128]{3,2,1,0:T(8,128)S(1)} %get-tuple-element.2) | data formatting | bytes 16777216
  223.2 3.4 %copy.11 = f32[16,32,32,128]{3,2,1,0:T(8,128)} copy(f32[16,32,32,128]{3,2,1,0:T(8,128)S(1)} %get-tuple-element.3) | data formatting | bytes 16777216

commit v4 on v3

--- a/solution.py
+++ b/solution.py
@@ -28,7 +28,7 @@
     ang = 2.0 * np.pi * ((idx[:, None] * idx[None, :]) % N) / N
     cos, sin = np.cos(ang) / math.sqrt(N), np.sin(ang) / math.sqrt(N)
     mat = np.stack([np.stack([cos, sin], 1), np.stack([-sin, cos], 1)])
-    fx = mat.reshape(2, NP, NJ, KC, 2 * N).transpose(1, 2, 0, 3, 4).reshape(2 * N, 2 * N)
+    fx = mat.reshape(2, NP, NJ, KC, 2 * N).transpose(2, 1, 0, 3, 4).reshape(2 * N, 2 * N)
     fy = mat.reshape(2, NP, B, 2, NP, B).transpose(1, 0, 2, 4, 3, 5).reshape(2 * N, 2 * N)
     fz = mat.transpose(2, 3, 0, 1).reshape(2 * N, 2 * N)
     return fx.astype(np.float32), fy.astype(np.float32), fz.astype(np.float32)
@@ -46,16 +46,16 @@
     y = code.astype(jnp.float32)
     p = jnp.maximum(jnp.abs(y), TINY)
     root = lax.rsqrt(lax.rsqrt(p * lax.rsqrt(p)))
-    return jnp.where(y < 0, -root, root) * scale
-
-
-def scale_of(peak):
-    return jnp.maximum(peak * 2.0 ** -15, TINY).astype(jnp.bfloat16).astype(jnp.float32)
+    return jnp.where(y == 0, 0.0, jnp.where(y < 0, -root, root)) * scale
+
+
+def scale_of(x):
+    return jnp.maximum(x, TINY).astype(jnp.bfloat16).astype(jnp.float32)
 
 
 def kernel(ng, fx_ref, fy_ref, fz_ref, g_ref, ur_ref, ui_ref, wr_ref, wi_ref,
-           stage, xout, xsend, xrecv, ysend, yrecv, scales,
-           in_sem, xs_sem, xr_sem, ys_sem, yr_sem):
+           stage, xout, xsend, xrecv, ysend, yrecv, ssend, srecv,
+           in_sem, xs_sem, xr_sem, ys_sem, yr_sem, ss_sem, sr_sem):
     nt = ng * NJ
     col, row = lax.axis_index("col"), lax.axis_index("row")
     highest = lax.Precision.HIGHEST
@@ -87,33 +87,56 @@
             src, yrecv.at[t, col], ys_sem.at[lax.rem(t, YS), d], yr_sem.at[t, col],
             device_id={"col": dst}, device_id_type=MESH)
 
+    def scale_copy(grp, d):
+        dst = peer(col, d)
+        src = ssend.at[grp]
+        if d == 0:
+            return pltpu.make_async_copy(src, srecv.at[grp, col], sr_sem.at[grp, col])
+        return pltpu.make_async_remote_copy(
+            src, srecv.at[grp, col], ss_sem.at[grp, d], sr_sem.at[grp, col],
+            device_id={"col": dst}, device_id_type=MESH)
+
     def arrived(buf, sem, t):
         for p in range(NP):
             pltpu.make_async_copy(buf.at[t, p], buf.at[t, p], sem.at[t, p]).wait()
 
-    def x_step(grp):
+    def row_scale(grp):
         slot = lax.rem(grp, 2)
         for copy in load(grp, slot):
             copy.wait()
 
-        def body(yy, peak):
+        def body(y, peaks):
+            blocks = [jnp.abs(stage[slot, :, f, pl.ds(y, 1)]).reshape(2 * B // 8, 8, N) for f in range(FG)]
+            return tuple(jnp.maximum(peak, jnp.max(block, axis=0)) for peak, block in zip(peaks, blocks))
+
+        peaks = lax.fori_loop(0, B, body, (jnp.zeros((8, N), jnp.float32),) * FG)
+        field = lax.broadcasted_iota(jnp.int32, (1, N), 1) // B
+        scale = jnp.zeros((1, N), jnp.float32)
+        for f, peak in enumerate(peaks):
+            peak = jnp.max(jnp.max(peak, axis=1, keepdims=True), axis=0, keepdims=True)
+            scale = jnp.where(field == f, peak, scale)
+        return scale_of(scale * 2.0 ** -11)
+
+    def x_step(grp, scale, lo, hi):
+        slot = lax.rem(grp, 2)
+
+        def body(yy, _):
             pieces = []
             for dy in range(2):
                 y = yy * 2 + dy
                 halves = [stage[slot, c, :, pl.ds(y, 1)].reshape(FG * B, N) for c in range(2)]
                 pieces.append(jnp.concatenate(halves, axis=1))
             data = jnp.concatenate(pieces, axis=0)
-            out = lax.dot_general(fx_ref[...], data, (((1,), (1,)), ((), ())), precision=highest,
+            rows = 2 * NP * KC
+            out = lax.dot_general(fx_ref[lo * rows:hi * rows, :], data, (((1,), (1,)), ((), ())), precision=highest,
                                   preferred_element_type=jnp.float32)
             for dy in range(2):
-                for blk in range(2 * NP * NJ):
-                    base = blk // 2 * MSG + blk % 2 * B + yy * 2 + dy
+                for blk in range((hi - lo) * NP * 2):
+                    base = (lo * NP + blk // 2) * MSG + blk % 2 * B + yy * 2 + dy
                     xout[pl.ds(base, KC, stride=2 * B), :] = out[blk * KC:(blk + 1) * KC, dy * N:(dy + 1) * N]
-            tall = jnp.max(jnp.abs(out).reshape(2 * N // 8, 8, 2 * N), axis=0)
-            return jnp.maximum(peak, jnp.maximum(tall[:, :N], tall[:, N:]))
-
-        peak = lax.fori_loop(0, B // 2, body, jnp.zeros((8, N), jnp.float32))
-        scale = scale_of(jnp.max(peak, axis=0, keepdims=True))
+            return 0
+
+        lax.fori_loop(0, B // 2, body, 0)
         tail = jnp.broadcast_to(scale, (SC, N)).astype(jnp.bfloat16)
 
         def send(j, _):
@@ -121,7 +144,7 @@
             place = lax.rem(t, 2 * NJ)
 
             def pack(r, _):
-                rows = pl.ds(pl.multiple_of((r * NJ + j) * MSG, MSG), MSG)
+                rows = pl.ds(pl.multiple_of((j * NP + r) * MSG, MSG), MSG)
                 xsend[place, r, :MSG, :] = encode(xout[rows, :], scale)
                 xsend[place, r, MSG:, :] = tail
                 return 0
@@ -131,7 +154,7 @@
                 row_copy(t, d).start()
             return 0
 
-        lax.fori_loop(0, NJ, send, 0)
+        lax.fori_loop(lo, hi, send, 0)
 
     def row_drained(grp):
         def body(j, _):
@@ -144,6 +167,16 @@
     def y_step(t):
         slot = lax.rem(t, YS)
         arrived(xrecv, xr_sem, t)
+        given = [xrecv[t, p, MSG:, :].astype(jnp.float32)[:1] for p in range(NP)]
+        scale = scale_of(4.0 * sum(given))
+
+        @pl.when(lax.rem(t, NJ) == 0)
+        def _():
+            ssend[t // NJ] = jnp.broadcast_to(scale, (SC, N)).astype(jnp.bfloat16)
+            for d in (2, 3, 1, 0):
+                scale_copy(t // NJ, d).start()
+
+        scale2 = jnp.concatenate([scale, scale], axis=1)
 
         def body(kk, _):
             cols = []
@@ -151,14 +184,12 @@
                 k = kk * 2 + dk
                 rows = pl.ds(pl.multiple_of(k * 2 * B, 2 * B), 2 * B)
                 cols.append(jnp.concatenate(
-                    [decode(xrecv[t, p, rows, :], xrecv[t, p, MSG:, :].astype(jnp.float32)[:1]) for p in range(NP)],
+                    [decode(xrecv[t, p, rows, :], given[p]) for p in range(NP)],
                     axis=0))
             data = jnp.concatenate(cols, axis=1)
             out = jnp.dot(fy_ref[...], data, precision=highest, preferred_element_type=jnp.float32)
-            scale = scale_of(jnp.max(jnp.abs(out), axis=0, keepdims=True))
-            out = encode(out, scale)
+            out = encode(out, scale2)
             for dk in range(2):
-                scales[pl.ds(kk * 2 + dk, 1), :] = scale[:, dk * N:(dk + 1) * N]
                 for s in range(NP):
                     for c in range(2):
                         rows = pl.ds(pl.multiple_of(c * KC * B + (kk * 2 + dk) * B, B), B)
@@ -166,27 +197,30 @@
             return 0
 
         lax.fori_loop(0, KC // 2, body, 0)
-        tail = jnp.concatenate([scales[...]] * (SC // KC), axis=0).astype(jnp.bfloat16)
-        for s in range(NP):
-            ysend[slot, s, MSG:MSG + SC, :] = tail
         for d in (2, 3, 1, 0):
             col_copy(t, d).start()
 
     def z_step(t):
         grp, j = t // NJ, lax.rem(t, NJ)
+        @pl.when(j == 0)
+        def _():
+            arrived(srecv, sr_sem, grp)
+
         arrived(yrecv, yr_sem, t)
         half = KC * B
         gain = g_ref[pl.ds(j * KC, KC)].reshape(half, N)
-        group = lax.broadcasted_iota(jnp.int32, (MSG + SC, N), 1) // B
-        for f in range(FG):
+        def take(f, pieces):
+            group = lax.broadcasted_iota(jnp.int32, pieces[0].shape, 1) // B
             code = None
-            for q in range(NP):
-                piece = yrecv[t, q]
+            for q, piece in enumerate(pieces):
                 if q != f:
                     piece = pltpu.roll(piece, (q - f) % NP * B, 1)
                 code = piece if code is None else jnp.where(group == q, piece, code)
-            rows = code[MSG:].astype(jnp.float32)
-            scale = jnp.concatenate([jnp.broadcast_to(rows[k:k + 1], (B, N)) for k in range(KC)], axis=0)
+            return code
+
+        for f in range(FG):
+            code = take(f, [yrecv[t, q] for q in range(NP)])
+            scale = take(f, [srecv[grp, q].astype(jnp.float32) for q in range(NP)])[:1]
             data = jnp.concatenate([decode(code[c * half:(c + 1) * half], scale) for c in range(2)], axis=1)
             out = jnp.dot(data, fz_ref[...], precision=highest, preferred_element_type=jnp.float32)
             for c, dst in enumerate((wr_ref, wi_ref)):
@@ -202,10 +236,9 @@
         pl.semaphore_signal(barrier, inc=1, device_id={"col": peer(col, d)}, device_id_type=MESH)
     pl.semaphore_wait(barrier, 2 * (NP - 1))
 
-    x_step(0)
-
-    if ng > 1:
-        x_step(1)
+    scale0 = row_scale(0)
+    x_step(0, scale0, 0, 1)
+    x_step(0, scale0, 1, NJ)
     if ng > 2:
         for copy in load(2, 0):
             copy.start()
@@ -218,6 +251,11 @@
 
         y_step(t)
 
+        if ng > 1:
+            @pl.when(t == 0)
+            def _():
+                x_step(1, row_scale(1), 0, NJ)
+
         @pl.when(t >= LAG)
         def _():
             z_step(t - LAG)
@@ -227,7 +265,7 @@
             def _():
                 grp = t // NJ
                 row_drained(grp)
-                x_step(grp + 2)
+                x_step(grp + 2, row_scale(grp + 2), 0, NJ)
 
                 @pl.when(grp + 3 < ng)
                 def _():
@@ -248,6 +286,9 @@
     for t in range(max(nt - YS, 0), nt):
         for d in (1, 2, 3):
             col_copy(t, d).wait_send()
+    for grp in range(ng):
+        for d in (1, 2, 3):
+            scale_copy(grp, d).wait_send()
 
 
 def solution(mesh):
@@ -270,14 +311,17 @@
                 pltpu.VMEM((NP * NJ * MSG, N), jnp.float32),
                 pltpu.VMEM((2 * NJ, NP, MSG + SC, N), jnp.bfloat16),
                 pltpu.VMEM((nt, NP, MSG + SC, N), jnp.bfloat16),
-                pltpu.VMEM((YS, NP, MSG + SC, N), jnp.bfloat16),
-                pltpu.VMEM((nt, NP, MSG + SC, N), jnp.bfloat16),
-                pltpu.VMEM((KC, N), jnp.float32),
+                pltpu.VMEM((YS, NP, MSG, N), jnp.bfloat16),
+                pltpu.VMEM((nt, NP, MSG, N), jnp.bfloat16),
+                pltpu.VMEM((ng, SC, N), jnp.bfloat16),
+                pltpu.VMEM((ng, NP, SC, N), jnp.bfloat16),
                 pltpu.SemaphoreType.DMA((2, 2)),
                 pltpu.SemaphoreType.DMA((2 * NJ, NP)),
                 pltpu.SemaphoreType.DMA((nt, NP)),
                 pltpu.SemaphoreType.DMA((YS, NP)),
                 pltpu.SemaphoreType.DMA((nt, NP)),
+                pltpu.SemaphoreType.DMA((ng, NP)),
+                pltpu.SemaphoreType.DMA((ng, NP)),
             ],
             compiler_params=pltpu.CompilerParams(
                 collective_id=0, has_side_effects=True, vmem_limit_bytes=44 << 20),

time: 227 us -> 220 us (0.969)
  Pallas kernels: 219 us -> 213 us
    pallas_call x1, Pallas kernels: 219 us -> 213 us  [local_forward(): pl.pallas_call(functools.partial(kernel, ng), out_shape=(out, out), in_sp...]
where the time goes in v4:
time: 220 us
  Pallas kernels  213 us (97%)
  local copies, waits for them, and re-layouts  6.8 us (3%)
    pallas_call x1, Pallas kernels, local_forward(): pl.pallas_call(functools.partial(kernel, ng), out_shape=(out, out), in_sp...  213 us
    unnamed x2, local copies, waits for them, and re-layouts  6.8 us

profile of v4, /device:TPU:0, one launch (start us, length us, event | category | flops | bytes accessed | tf_op | source)
XLA Modules:
  0.0 220.1 jit_solution(4630754337367768866)
XLA Ops:
  0.6 212.6 %shard_map.77 = (f32[16,32,32,128]{3,2,1,0:T(8,128)S(1)}, f32[16,32,32,128]{3,2,1,0:T(8,128)S(1)}) custom-call(f32[256,256]{1,0:T(8,128)} %constant.6.clone.fx_ref, f32[256,256]{1,0:T(8,128)} %constant.7.clone.fy_ref, f32[256,256]{1,0:T(8,128)} %constant.8.clone.fz_ref, f32[32,32,128]{2,1,0:T(8,128)} %g_ref.1, f32[16,32,32,128]{3,2,1,0:T(8,128)} %bitcast.2, ...), custom_call_target="tpu_custom_call" | custom-call | flops 51539607552 | bytes 33554432 | tf_op jit(solution)/shard_map/pallas_call | solution.py:304
  213.3 3.4 %copy.10 = f32[16,32,32,128]{3,2,1,0:T(8,128)} copy(f32[16,32,32,128]{3,2,1,0:T(8,128)S(1)} %get-tuple-element.2) | data formatting | bytes 16777216
  216.7 3.4 %copy.11 = f32[16,32,32,128]{3,2,1,0:T(8,128)} copy(f32[16,32,32,128]{3,2,1,0:T(8,128)S(1)} %get-tuple-element.3) | data formatting | bytes 16777216

commit v5 on v4

--- a/solution.py
+++ b/solution.py
@@ -53,7 +53,48 @@
     return jnp.maximum(x, TINY).astype(jnp.bfloat16).astype(jnp.float32)
 
 
-def kernel(ng, fx_ref, fy_ref, fz_ref, g_ref, ur_ref, ui_ref, wr_ref, wi_ref,
+def take(f, pieces):
+    group = lax.broadcasted_iota(jnp.int32, pieces[0].shape, 1) // B
+    code = None
+    for q, piece in enumerate(pieces):
+        if q != f:
+            piece = pltpu.roll(piece, (q - f) % NP * B, 1)
+        code = piece if code is None else jnp.where(group == q, piece, code)
+    return code
+
+
+def z_field(f, codes, scales, fz_ref, gain):
+    half = KC * B
+    code = take(f, codes)
+    scale = take(f, [s.astype(jnp.float32) for s in scales])[:1]
+    data = jnp.concatenate([decode(code[c * half:(c + 1) * half], scale) for c in range(2)], axis=1)
+    out = jnp.dot(data, fz_ref[...], precision=lax.Precision.HIGHEST, preferred_element_type=jnp.float32)
+    return [(out[:, c * N:(c + 1) * N] * gain).reshape(KC, B, N) for c in range(2)]
+
+
+def finish(ng, fz_ref, g_ref, wr_ref, wi_ref, code_ref, scale_ref, or_ref, oi_ref, stage, sem, last_sem):
+    kx, done = (NJ - 1) * KC, (ng - 1) * FG
+    copies = []
+    for c, (src, dst) in enumerate(((wr_ref, or_ref), (wi_ref, oi_ref))):
+        tail = (pl.ds(done, FG), pl.ds(0, kx))
+        copies.append(pltpu.make_async_copy(src.at[tail], dst.at[tail], sem.at[c, 0]))
+        if done:
+            copies.append(pltpu.make_async_copy(src.at[pl.ds(0, done)], dst.at[pl.ds(0, done)], sem.at[c, 1]))
+    for copy in copies:
+        copy.start()
+    gain = g_ref[kx:].reshape(KC * B, N)
+    for f in range(FG):
+        parts = z_field(f, [code_ref[q] for q in range(NP)], [scale_ref[q] for q in range(NP)], fz_ref, gain)
+        for c, (part, dst) in enumerate(zip(parts, (or_ref, oi_ref))):
+            stage[c, f] = part
+            copy = pltpu.make_async_copy(stage.at[c, f], dst.at[done + f, pl.ds(kx, KC)], last_sem.at[c, f])
+            copy.start()
+            copies.append(copy)
+    for copy in copies:
+        copy.wait()
+
+
+def kernel(ng, fx_ref, fy_ref, fz_ref, g_ref, ur_ref, ui_ref, wr_ref, wi_ref, code_ref, scale_ref,
            stage, xout, xsend, xrecv, ysend, yrecv, ssend, srecv,
            in_sem, xs_sem, xr_sem, ys_sem, yr_sem, ss_sem, sr_sem):
     nt = ng * NJ
@@ -197,8 +238,16 @@
             return 0
 
         lax.fori_loop(0, KC // 2, body, 0)
-        for d in (2, 3, 1, 0):
-            col_copy(t, d).start()
+        @pl.when(t < nt - 1)
+        def _():
+            for d in (2, 3, 1, 0):
+                col_copy(t, d).start()
+
+        @pl.when(t == nt - 1)
+        def _():
+            for d in (1, 2, 3, 0):
+                col_copy(t, d).start()
+
 
     def z_step(t):
         grp, j = t // NJ, lax.rem(t, NJ)
@@ -207,24 +256,11 @@
             arrived(srecv, sr_sem, grp)
 
         arrived(yrecv, yr_sem, t)
-        half = KC * B
-        gain = g_ref[pl.ds(j * KC, KC)].reshape(half, N)
-        def take(f, pieces):
-            group = lax.broadcasted_iota(jnp.int32, pieces[0].shape, 1) // B
-            code = None
-            for q, piece in enumerate(pieces):
-                if q != f:
-                    piece = pltpu.roll(piece, (q - f) % NP * B, 1)
-                code = piece if code is None else jnp.where(group == q, piece, code)
-            return code
-
+        gain = g_ref[pl.ds(j * KC, KC)].reshape(KC * B, N)
         for f in range(FG):
-            code = take(f, [yrecv[t, q] for q in range(NP)])
-            scale = take(f, [srecv[grp, q].astype(jnp.float32) for q in range(NP)])[:1]
-            data = jnp.concatenate([decode(code[c * half:(c + 1) * half], scale) for c in range(2)], axis=1)
-            out = jnp.dot(data, fz_ref[...], precision=highest, preferred_element_type=jnp.float32)
-            for c, dst in enumerate((wr_ref, wi_ref)):
-                dst[grp * FG + f, pl.ds(j * KC, KC)] = (out[:, c * N:(c + 1) * N] * gain).reshape(KC, B, N)
+            parts = z_field(f, [yrecv[t, q] for q in range(NP)], [srecv[grp, q] for q in range(NP)], fz_ref, gain)
+            for part, dst in zip(parts, (wr_ref, wi_ref)):
+                dst[grp * FG + f, pl.ds(j * KC, KC)] = part
 
     for grp in range(min(2, ng)):
         for copy in load(grp, grp):
@@ -252,7 +288,7 @@
         y_step(t)
 
         if ng > 1:
-            @pl.when(t == 0)
+            @pl.when(t == 1)
             def _():
                 x_step(1, row_scale(1), 0, NJ)
 
@@ -280,7 +316,11 @@
         z_step(t)
         return 0
 
-    lax.fori_loop(max(nt - LAG, 0), nt, drain, 0)
+    lax.fori_loop(max(nt - LAG, 0), nt - 1, drain, 0)
+    arrived(yrecv, yr_sem, nt - 1)
+    for q in range(NP):
+        code_ref[q] = yrecv[nt - 1, q]
+        scale_ref[q] = srecv[ng - 1, q]
     for grp in range(max(ng - 2, 0), ng):
         row_drained(grp)
     for t in range(max(nt - YS, 0), nt):
@@ -301,11 +341,11 @@
         out = pltpu.VMEM((ng * FG, B, B, N), jnp.float32)
         vmem, anywhere = pl.BlockSpec(memory_space=pltpu.VMEM), pl.BlockSpec(memory_space=pl.ANY)
         flops = 2 * 2 * N * 2 * N * N * B * B // N * ng * FG * 24
-        return pl.pallas_call(
+        w_real, w_imag, code, scale = pl.pallas_call(
             functools.partial(kernel, ng),
-            out_shape=(out, out),
+            out_shape=(out, out, pltpu.VMEM((NP, MSG, N), jnp.bfloat16), pltpu.VMEM((NP, SC, N), jnp.bfloat16)),
             in_specs=[vmem] * 4 + [anywhere] * 2,
-            out_specs=(vmem, vmem),
+            out_specs=(vmem,) * 4,
             scratch_shapes=[
                 pltpu.VMEM((2, 2, FG, B, B, N), jnp.float32),
                 pltpu.VMEM((NP * NJ * MSG, N), jnp.float32),
@@ -327,6 +367,19 @@
                 collective_id=0, has_side_effects=True, vmem_limit_bytes=44 << 20),
             cost_estimate=pl.CostEstimate(flops=flops, bytes_accessed=1 << 25, transcendentals=0),
         )(jnp.asarray(fx), jnp.asarray(fy), jnp.asarray(fz), g_filter, u_real, u_imag)
+        result = jax.ShapeDtypeStruct((ng * FG, B, B, N), jnp.float32)
+        return pl.pallas_call(
+            functools.partial(finish, ng),
+            out_shape=(result, result),
+            in_specs=[vmem] * 6,
+            out_specs=(anywhere, anywhere),
+            scratch_shapes=[
+                pltpu.VMEM((2, FG, KC, B, N), jnp.float32),
+                pltpu.SemaphoreType.DMA((2, 2)),
+                pltpu.SemaphoreType.DMA((2, FG)),
+            ],
+            compiler_params=pltpu.CompilerParams(vmem_limit_bytes=16 << 20),
+        )(jnp.asarray(fz), g_filter, w_real, w_imag, code, scale)
 
     field_spec = P("fld", None, "row", "col")
     out_spec = P("fld", "row", "col", None)

time: 220 us -> 216 us (0.982)
  local copies, waits for them, and re-layouts: 6.8 us -> 0.01 us
  Pallas kernels: 213 us -> 216 us
    unnamed x2 -> x4, local copies, waits for them, and re-layouts: 6.8 us -> 0.01 us
    pallas_call x1 -> x2, Pallas kernels: 213 us -> 216 us  [the longest x1 209 us: local_forward(): pl.pallas_call(functools.partial(kernel, ng), out_shape=(out, out, pltpu....]
where the time goes in v5:
time: 216 us
  Pallas kernels  216 us (100%)
    pallas_call x1, Pallas kernels, local_forward(): pl.pallas_call(functools.partial(kernel, ng), out_shape=(out, out, pltpu....  209 us
    pallas_call x1, Pallas kernels, local_forward(): pl.pallas_call(functools.partial(finish, ng), out_shape=(result, result),...  6.65 us

profile of v5, /device:TPU:0, one launch (start us, length us, event | category | flops | bytes accessed | tf_op | source)
XLA Modules:
  0.0 216.2 jit_solution(9105305387459838959)
XLA Ops:
  0.6 0.0 copy-start
  0.6 0.0 copy-start.1
  0.7 208.9 %shard_map.77 = (f32[16,32,32,128]{3,2,1,0:T(8,128)S(1)}, f32[16,32,32,128]{3,2,1,0:T(8,128)S(1)}, bf16[4,512,128]{2,1,0:T(8,128)(2,1)S(1)}, bf16[4,16,128]{2,1,0:T(8,128)(2,1)S(1)}) custom-call(f32[256,256]{1,0:T(8,128)} %constant.6.clone.fx_ref, f32[256,256]{1,0:T(8,128)} %constant.7.clone.fy_ref, f32[256,256]{1,0:T(8,128)} %constant.8.clone.fz_ref, ...), custom_call_target="tpu_custom_call" | custom-call | flops 51539607552 | bytes 33554432 | tf_op jit(solution)/shard_map/pallas_call | solution.py:344
  209.6 0.0 copy-done
  209.6 0.0 copy-done.1
  209.6 6.7 %shard_map.78 = (f32[16,32,32,128]{3,2,1,0:T(8,128)}, f32[16,32,32,128]{3,2,1,0:T(8,128)}) custom-call(f32[256,256]{1,0:T(8,128)S(1)} %copy-done.1, f32[32,32,128]{2,1,0:T(8,128)S(1)} %copy-done, f32[16,32,32,128]{3,2,1,0:T(8,128)S(1)} %get-tuple-element.6.wr_ref, f32[16,32,32,128]{3,2,1,0:T(8,128)S(1)} %get-tuple-element.7.wi_ref, ...), custom_call_target="tpu_custom_call" | custom-call | tf_op jit(solution)/shard_map/pallas_call | solution.py:371
Async XLA Ops:
  0.6 208.9 %copy-start = (f32[32,32,128]{2,1,0:T(8,128)S(1)}, f32[32,32,128]{2,1,0:T(8,128)}, u32[]{:S(2)}) copy-start(f32[32,32,128]{2,1,0:T(8,128)} %g_ref.3) | copy-start | bytes 1572868
  0.6 208.9 %copy-start.1 = (f32[256,256]{1,0:T(8,128)S(1)}, f32[256,256]{1,0:T(8,128)}, u32[]{:S(2)}) copy-start(f32[256,256]{1,0:T(8,128)} %constant.8.clone.fz_ref) | copy-start | bytes 786436

commit v6 on v5

--- a/solution.py
+++ b/solution.py
@@ -14,12 +14,12 @@
 B = 32
 NP = 4
 FG = 4
-KC = 8
+KC = 4
 NJ = B // KC
 MSG = 2 * KC * B
 SC = 16
 TINY = 2.0 ** -126
-LAG = 6
+LAG = 12
 YS = LAG + 2
 
 
@@ -158,7 +158,7 @@
             scale = jnp.where(field == f, peak, scale)
         return scale_of(scale * 2.0 ** -11)
 
-    def x_step(grp, scale, lo, hi):
+    def x_step(grp, scale, lo, hi, before_send=None):
         slot = lax.rem(grp, 2)
 
         def body(yy, _):
@@ -179,6 +179,8 @@
 
         lax.fori_loop(0, B // 2, body, 0)
         tail = jnp.broadcast_to(scale, (SC, N)).astype(jnp.bfloat16)
+        if before_send is not None:
+            before_send()
 
         def send(j, _):
             t = grp * NJ + j
@@ -270,10 +272,9 @@
     for d in range(1, NP):
         pl.semaphore_signal(barrier, inc=1, device_id={"row": peer(row, d)}, device_id_type=MESH)
         pl.semaphore_signal(barrier, inc=1, device_id={"col": peer(col, d)}, device_id_type=MESH)
-    pl.semaphore_wait(barrier, 2 * (NP - 1))
 
     scale0 = row_scale(0)
-    x_step(0, scale0, 0, 1)
+    x_step(0, scale0, 0, 1, lambda: pl.semaphore_wait(barrier, 2 * (NP - 1)))
     x_step(0, scale0, 1, NJ)
     if ng > 2:
         for copy in load(2, 0):
@@ -288,7 +289,7 @@
         y_step(t)
 
         if ng > 1:
-            @pl.when(t == 1)
+            @pl.when(t == NJ - 3)
             def _():
                 x_step(1, row_scale(1), 0, NJ)
 

time: 216 us -> 217 us (level)
  no operation moved by 1% of the time
where the time goes in v6:
time: 217 us
  Pallas kernels  216 us (100%)
    pallas_call x1, Pallas kernels, local_forward(): pl.pallas_call(functools.partial(kernel, ng), out_shape=(out, out, pltpu....  210 us
    pallas_call x1, Pallas kernels, local_forward(): pl.pallas_call(functools.partial(finish, ng), out_shape=(result, result),...  6.43 us

profile of v6, /device:TPU:0, one launch (start us, length us, event | category | flops | bytes accessed | tf_op | source)
XLA Modules:
  0.0 216.8 jit_solution(8153662025377303828)
XLA Ops:
  0.6 0.0 copy-start
  0.6 0.0 copy-start.1
  0.7 209.7 %shard_map.77 = (f32[16,32,32,128]{3,2,1,0:T(8,128)S(1)}, f32[16,32,32,128]{3,2,1,0:T(8,128)S(1)}, bf16[4,256,128]{2,1,0:T(8,128)(2,1)S(1)}, bf16[4,16,128]{2,1,0:T(8,128)(2,1)S(1)}) custom-call(f32[256,256]{1,0:T(8,128)} %constant.6.clone.fx_ref, f32[256,256]{1,0:T(8,128)} %constant.7.clone.fy_ref, f32[256,256]{1,0:T(8,128)} %constant.8.clone.fz_ref, ...), custom_call_target="tpu_custom_call" | custom-call | flops 51539607552 | bytes 33554432 | tf_op jit(solution)/shard_map/pallas_call | solution.py:345
  210.4 0.0 copy-done
  210.4 0.0 copy-done.1
  210.4 6.4 %shard_map.78 = (f32[16,32,32,128]{3,2,1,0:T(8,128)}, f32[16,32,32,128]{3,2,1,0:T(8,128)}) custom-call(f32[256,256]{1,0:T(8,128)S(1)} %copy-done.1, f32[32,32,128]{2,1,0:T(8,128)S(1)} %copy-done, f32[16,32,32,128]{3,2,1,0:T(8,128)S(1)} %get-tuple-element.6.wr_ref, f32[16,32,32,128]{3,2,1,0:T(8,128)S(1)} %get-tuple-element.7.wi_ref, ...), custom_call_target="tpu_custom_call" | custom-call | tf_op jit(solution)/shard_map/pallas_call | solution.py:372
Async XLA Ops:
  0.6 209.8 %copy-start = (f32[32,32,128]{2,1,0:T(8,128)S(1)}, f32[32,32,128]{2,1,0:T(8,128)}, u32[]{:S(2)}) copy-start(f32[32,32,128]{2,1,0:T(8,128)} %g_ref.3) | copy-start | bytes 1572868
  0.6 209.8 %copy-start.1 = (f32[256,256]{1,0:T(8,128)S(1)}, f32[256,256]{1,0:T(8,128)}, u32[]{:S(2)}) copy-start(f32[256,256]{1,0:T(8,128)} %constant.8.clone.fz_ref) | copy-start | bytes 786436

commit v7 on v6

--- a/solution.py
+++ b/solution.py
@@ -14,13 +14,14 @@
 B = 32
 NP = 4
 FG = 4
-KC = 4
+KC = 8
 NJ = B // KC
 MSG = 2 * KC * B
 SC = 16
 TINY = 2.0 ** -126
-LAG = 12
-YS = LAG + 2
+LAG = 8
+HOLD = 3
+YS = LAG + HOLD + 2
 
 
 def dft_tables():
@@ -240,16 +241,28 @@
             return 0
 
         lax.fori_loop(0, KC // 2, body, 0)
-        @pl.when(t < nt - 1)
-        def _():
-            for d in (2, 3, 1, 0):
+        col_copy(t, 0).start()
+        at_end = (col == 0) | (col == NP - 1)
+
+        @pl.when(at_end)
+        def _():
+            col_copy(t, 1).start()
+
+            @pl.when(t >= HOLD)
+            def _():
+                for d in (2, 3):
+                    col_copy(t - HOLD, d).start()
+
+            @pl.when(t == nt - 1)
+            def _():
+                for late in range(nt - min(HOLD, nt), nt):
+                    for d in (2, 3):
+                        col_copy(late, d).start()
+
+        @pl.when(jnp.logical_not(at_end))
+        def _():
+            for d in (2, 3, 1):
                 col_copy(t, d).start()
-
-        @pl.when(t == nt - 1)
-        def _():
-            for d in (1, 2, 3, 0):
-                col_copy(t, d).start()
-
 
     def z_step(t):
         grp, j = t // NJ, lax.rem(t, NJ)
@@ -365,7 +378,7 @@
                 pltpu.SemaphoreType.DMA((ng, NP)),
             ],
             compiler_params=pltpu.CompilerParams(
-                collective_id=0, has_side_effects=True, vmem_limit_bytes=44 << 20),
+                collective_id=0, has_side_effects=True, vmem_limit_bytes=46 << 20),
             cost_estimate=pl.CostEstimate(flops=flops, bytes_accessed=1 << 25, transcendentals=0),
         )(jnp.asarray(fx), jnp.asarray(fy), jnp.asarray(fz), g_filter, u_real, u_imag)
         result = jax.ShapeDtypeStruct((ng * FG, B, B, N), jnp.float32)

time: 217 us -> 225 us (1.037)
  Pallas kernels: 216 us -> 223 us
    pallas_call x1, Pallas kernels: 210 us -> 216 us  [local_forward(): pl.pallas_call(functools.partial(kernel, ng), out_shape=(out, out, pltpu....]
where the time goes in v7:
time: 225 us; the launch traced here: 223 us
  Pallas kernels  223 us (99%)
    pallas_call x1, Pallas kernels, local_forward(): pl.pallas_call(functools.partial(kernel, ng), out_shape=(out, out, pltpu....  216 us
    pallas_call x1, Pallas kernels, local_forward(): pl.pallas_call(functools.partial(finish, ng), out_shape=(result, result),...  6.65 us

profile of v7, /device:TPU:0, one launch (start us, length us, event | category | flops | bytes accessed | tf_op | source)
XLA Modules:
  0.0 223.4 jit_solution(5277982954430141820)
XLA Ops:
  0.6 0.0 copy-start
  0.6 0.0 copy-start.1
  0.7 216.1 %shard_map.77 = (f32[16,32,32,128]{3,2,1,0:T(8,128)S(1)}, f32[16,32,32,128]{3,2,1,0:T(8,128)S(1)}, bf16[4,512,128]{2,1,0:T(8,128)(2,1)S(1)}, bf16[4,16,128]{2,1,0:T(8,128)(2,1)S(1)}) custom-call(f32[256,256]{1,0:T(8,128)} %constant.6.clone.fx_ref, f32[256,256]{1,0:T(8,128)} %constant.7.clone.fy_ref, f32[256,256]{1,0:T(8,128)} %constant.8.clone.fz_ref, ...), custom_call_target="tpu_custom_call" | custom-call | flops 51539607552 | bytes 33554432 | tf_op jit(solution)/shard_map/pallas_call | solution.py:358
  216.7 0.0 copy-done
  216.7 0.0 copy-done.1
  216.8 6.7 %shard_map.78 = (f32[16,32,32,128]{3,2,1,0:T(8,128)}, f32[16,32,32,128]{3,2,1,0:T(8,128)}) custom-call(f32[256,256]{1,0:T(8,128)S(1)} %copy-done.1, f32[32,32,128]{2,1,0:T(8,128)S(1)} %copy-done, f32[16,32,32,128]{3,2,1,0:T(8,128)S(1)} %get-tuple-element.6.wr_ref, f32[16,32,32,128]{3,2,1,0:T(8,128)S(1)} %get-tuple-element.7.wi_ref, ...), custom_call_target="tpu_custom_call" | custom-call | tf_op jit(solution)/shard_map/pallas_call | solution.py:385
Async XLA Ops:
  0.6 216.1 %copy-start = (f32[32,32,128]{2,1,0:T(8,128)S(1)}, f32[32,32,128]{2,1,0:T(8,128)}, u32[]{:S(2)}) copy-start(f32[32,32,128]{2,1,0:T(8,128)} %g_ref.3) | copy-start | bytes 1572868
  0.6 216.1 %copy-start.1 = (f32[256,256]{1,0:T(8,128)S(1)}, f32[256,256]{1,0:T(8,128)}, u32[]{:S(2)}) copy-start(f32[256,256]{1,0:T(8,128)} %constant.8.clone.fz_ref) | copy-start | bytes 786436
